TPU v7x, 256 devices: a 2x2x32 block of a 4x8x32 slice. The times are simulated.
256 devices in a mesh: parts: 4 (over x, y), pts: 64 (over z, core).
Axes of the slice: x: 2, y: 2, z: 32, core: 2. Of those that a mesh axis runs over, the one named last changes fastest.
The devices are a block of a 4x8x32 slice.
Arguments:
- grid_weights: float32 [512, 128, 128], P(('parts', 'pts')), parts along dimension 0, may hold values from -6 to 6
- direction: float32 [512, 128, 128], P(('parts', 'pts')), parts along dimension 0, may hold values from -6 to 6
- kern_x: float32 [128, 128], replicated
- kern_y: float32 [128, 128], replicated
- kern_z: float32 [128, 128], replicated
- interp: bfloat16 [32768, 128, 256], P(('parts', 'pts')), parts along dimension 0, may hold values from -4 to 4
- block_corner: int32 [3, 32768], P(None, ('parts', 'pts')), parts along dimension 1, may hold values from 0 to 120, as said below
- block_offsets: int32 [32768, 256], P(('parts', 'pts')), parts along dimension 0, may hold values from 0 to 2047, as said below
- labels: int32 [32768, 128], P(('parts', 'pts')), parts along dimension 0, may hold values 0 or 1
- trial_steps: float32 [5], replicated, may hold values from 0.05 to 2
- accept: int32 [1], replicated, may hold values from 0 to 4
Outputs:
- new_weights: float32 [512, 128, 128], P(('parts', 'pts')), parts along dimension 0
- grid_gradient: float32 [512, 128, 128], P(('parts', 'pts')), parts along dimension 0
- curvature: float32 [32768, 128], P(('parts', 'pts')), parts along dimension 0
- trial_objective: float32 [20], P('parts'), parts along dimension 0
- trial_slope: float32 [20], P('parts'), parts along dimension 0
There are 4 independent parts, one for each index of `parts`. A program takes and returns all parts, laid end to end along the dimension named above; an argument that names none is the same for every part. Nothing has to cross between parts.
Inputs may be any that keep to these rules, and one draw needn't show every extreme that they name: `block_corner`: row 0 lies in 0 to 112, row 1 in 0 to 112, row 2 in 0 to 120. `block_offsets`: the 256 offsets of one block are distinct.
All inputs are finite; a program needn't handle non-finite values. No bound on the sum of `labels` on one device may be relied on, other than what follows from the above.
Results may differ from a plain program's by a relative error of at most 0.0075.
The roundings to bfloat16 on the way count: a program that leaves them out, or rounds other values in their place, can miss the bound.
Values may be sent and summed in bfloat16 or wider, within the bound.
No kernel may reach another device: no remote copies, remote signals or barrier semaphores. Data moves between devices by JAX's collectives and lax.ppermute only.
A program may use at most 128 MiB of HBM per device.

v0:
```python
import jax
import jax.numpy as jnp
from jax import lax
from jax.sharding import Mesh
from jax.sharding import PartitionSpec as P

BOXY = 16
BOXZ = 8
NTRIAL = 5
PTS = ("pts_0", "pts_1")
PARTS_PTS = ("parts", "pts_0", "pts_1")


HIGHEST = lax.Precision.HIGHEST


def by_axis(array, axes):
    for axis in axes:
        array = lax.psum(array, axis)
    return array


def sum_in_order(tiles, axes, order):
    inside = tiles.shape[1:]
    tiles = tiles.reshape(*(lax.axis_size(a) for a in axes), *inside)
    tiles = jnp.moveaxis(tiles, order, range(len(axes))).reshape(-1, *inside)
    for k in order:
        tiles = lax.psum_scatter(tiles, axes[k], scatter_dimension=0, tiled=True)
    return tiles[0]


def in_blocks(array, dim, count):
    lengths = array.shape
    tiles = array.reshape(*lengths[:dim], count, lengths[dim] // count, *lengths[dim + 1 :])
    return jnp.moveaxis(tiles, dim, 0)


def scatter_axes(array, axes, order, dim):
    count = lax.axis_size(axes)
    return sum_in_order(in_blocks(array, dim, count), axes, order)


def plane_mix(fields, kern_y, kern_z):
    inner_mix = jnp.einsum("...bc,zc->...bz", fields, kern_z, precision=HIGHEST)
    return jnp.einsum("...xbz,yb->...xyz", inner_mix, kern_y, precision=HIGHEST).astype(
        jnp.bfloat16
    )


def depth_mix(partial_value, kern_x):
    return jnp.einsum(
        "xa,...ayz->...xyz", kern_x, partial_value.astype(jnp.float32), precision=HIGHEST
    )


def cell_parts_of(block_corner, block_offsets, size_y):
    plane_off = block_offsets // (BOXY * BOXZ)
    row_off = block_offsets // BOXZ % BOXY
    depth_off = block_offsets % BOXZ
    cell_x = block_corner[0][:, None] + plane_off
    cell_y = block_corner[1][:, None] + row_off
    cell_z = block_corner[2][:, None] + depth_off
    return (cell_x * size_y + cell_y, cell_z)


def pick_cells(grid_rows, row_ids, depth_ids):
    depth_size = grid_rows.shape[-1]
    taken = jnp.take(grid_rows, row_ids, axis=1)
    depth_line = lax.broadcasted_iota(jnp.int32, (1, 1, depth_size), 2)
    wanted = depth_ids[:, :, None] == depth_line
    kept = jnp.where(wanted[None], taken, jnp.zeros((), taken.dtype))
    return jnp.sum(kept.astype(jnp.float32), axis=-1).astype(jnp.bfloat16)


def slab_add(row_ids, depth_ids, flat_terms, row_count, size_y, size_z):
    inside = (row_ids >= 0) & (row_ids < row_count * size_y)
    target_row = jnp.where(inside, row_ids, row_count * size_y)
    depth_line = lax.broadcasted_iota(jnp.int32, (1, size_z), 1)
    placed = jnp.where(depth_ids[:, None] == depth_line, flat_terms[:, None], 0.0)
    summed = (
        jnp.zeros((row_count * size_y, size_z), jnp.float32).at[target_row].add(placed, mode="drop")
    )
    return summed.reshape(row_count, size_y, size_z)


def kron_apply(fields, kern_x, kern_y, kern_z):
    partial_value = plane_mix(fields, kern_y, kern_z)
    slab_rows = fields.shape[1]
    gathered = lax.all_gather(partial_value, PTS, axis=1, tiled=True)
    mixed_grid = depth_mix(gathered, kern_x)
    slab_part = lax.dynamic_slice_in_dim(mixed_grid, lax.axis_index(PTS) * slab_rows, slab_rows, 1)
    return (slab_part, mixed_grid.astype(jnp.bfloat16))


def body(
    grid_weights,
    direction,
    kern_x,
    kern_y,
    kern_z,
    interp,
    block_corner,
    block_offsets,
    labels,
    trial_steps,
    accept,
):
    slab_rows, size_y, size_z = grid_weights.shape
    devices = lax.axis_size(PTS)
    points = interp.shape[0] * interp.shape[1] * devices
    row_ids, depth_ids = cell_parts_of(block_corner, block_offsets, size_y)
    slab_pair, whole_pair = kron_apply(jnp.stack([grid_weights, direction]), kern_x, kern_y, kern_z)
    quad_local = jnp.stack(
        [
            jnp.sum(grid_weights * slab_pair[0]),
            jnp.sum(direction * slab_pair[0]),
            jnp.sum(direction * slab_pair[1]),
        ]
    )
    values = pick_cells(whole_pair.reshape(2, -1, size_z), row_ids, depth_ids)
    latent_pair = jnp.einsum("bpc,fbc->fbp", interp, values, preferred_element_type=jnp.float32)
    latent = latent_pair[0]
    slope_pt = latent_pair[1]
    target = labels.astype(jnp.float32)
    signed = 2.0 * target - 1.0
    trial_latent = latent[None] + trial_steps[:, None, None] * slope_pt[None]
    loglik_local = jnp.sum(jax.nn.log_sigmoid(signed[None] * trial_latent), axis=(1, 2))
    descent_local = jnp.sum(
        (target[None] - jax.nn.sigmoid(trial_latent)) * slope_pt[None], axis=(1, 2)
    )
    quadratics, loglik, descent = (
        by_axis(quad_local, PTS),
        by_axis(loglik_local, PTS),
        by_axis(descent_local, PTS),
    )
    prior = 0.5 * (
        quadratics[0]
        + 2.0 * trial_steps * quadratics[1]
        + trial_steps * trial_steps * quadratics[2]
    )
    trial_objective = (loglik - prior) / points
    trial_slope = (descent - quadratics[1] - trial_steps * quadratics[2]) / points
    chosen = jnp.sum(jnp.where(jnp.arange(NTRIAL) == accept[0], trial_steps, 0.0))
    probability = jax.nn.sigmoid(latent + chosen * slope_pt)
    residual = (target - probability).astype(jnp.bfloat16)
    column_term = jnp.einsum("bpc,bp->bc", interp, residual, preferred_element_type=jnp.float32)
    flat_rows = row_ids.reshape(-1)
    flat_depths = depth_ids.reshape(-1)
    flat_terms = column_term.reshape(-1)
    spread = scatter_axes(
        slab_add(
            flat_rows, flat_depths, flat_terms, slab_rows * lax.axis_size(PTS), size_y, size_z
        ),
        PTS,
        (1, 0),
        0,
    )
    new_weights = grid_weights + chosen * direction
    grid_gradient = spread - new_weights
    unused_slab, bend_whole = kron_apply(grid_gradient[None], kern_x, kern_y, kern_z)
    bend_values = pick_cells(bend_whole.reshape(1, -1, size_z), row_ids, depth_ids)
    bend_pt = jnp.einsum("bpc,fbc->fbp", interp, bend_values, preferred_element_type=jnp.float32)[0]
    curvature = probability * (1.0 - probability) * bend_pt
    return (new_weights, grid_gradient, curvature, trial_objective, trial_slope)


def solution(mesh):
    finer = Mesh(mesh.devices.reshape(mesh.shape["parts"], 32, 2), ("parts", "pts_0", "pts_1"))
    placed = (
        P(PARTS_PTS, None, None),
        P(PARTS_PTS, None, None),
        P(),
        P(),
        P(),
        P(PARTS_PTS, None, None),
        P(None, PARTS_PTS),
        P(PARTS_PTS, None),
        P(PARTS_PTS, None),
        P(),
        P(),
    )
    return jax.shard_map(
        body,
        mesh=finer,
        in_specs=placed,
        out_specs=(
            P(PARTS_PTS, None, None),
            P(PARTS_PTS, None, None),
            P(PARTS_PTS, None),
            P("parts"),
            P("parts"),
        ),
        check_vma=False,
    )
```

profile of v0, /device:TPU:37, one launch (start us, length us, event | category | flops | bytes accessed | tf_op | source)
XLA Modules:
  0.0 1211.0 jit_solution(13192357690105287026)
XLA Ops:
  7.3 1.4 fusion.22
  8.6 1.9 fusion.19
  14.6 1.3 fusion.53
  16.9 6.4 iota_compare_fusion.1
  23.6 138.8 %all-gather.3.cloned.1.call-done = bf16[2,128,128,128]{2,3,1,0:T(8,128)(2,1)} async-done(((bf16[2,2,128,128]{2,3,1,0:T(8,128)(2,1)}), bf16[2,128,128,128]{2,3,1,0:T(8,128)(2,1)}) %all-gather.3.cloned.1.call-update) | async-done | bytes 8388624 | tf_op jit(solution)/shard_map/all_gather | solution.py:89
  162.4 12.4 %copy.56 = bf16[2,128,128,128]{3,1,2,0:T(8,128)(2,1)} copy(bf16[2,128,128,128]{2,3,1,0:T(8,128)(2,1)} %all-gather.3.cloned.1.call-done) | data formatting | bytes 16777216 | tf_op jit(solution)/shard_map/all_gather | solution.py:89
  174.8 9.8 fusion.42
  184.6 5.7 copy-done.1
  190.3 4.1 convert_bitcast_fusion
  194.4 12.0 copy.57
  206.4 16.4 %copy.58 = bf16[2,16384,128]{2,0,1:T(2,128)(2,1)} copy(bf16[2,16384,128]{2,1,0:T(8,128)(2,1)} %bitcast.127) | data formatting | bytes 16777216 | tf_op jit(solution)/shard_map/reshape | solution.py:120
  222.8 214.7 %gather_fusion = bf16[32768,2,128]{2,1,0:T(2,128)(2,1)} fusion(bf16[2,16384,128]{2,0,1:T(2,128)(2,1)} %copy.58, s32[32768]{0:T(1024)S(1)} %broadcast_clamp_fusion), kind=kCustom, calls=%fused_computation | custom fusion | bytes 33685504 | tf_op jit(solution)/shard_map/jit(_take)/gather | solution.py:68
  437.5 97.9 %fusion.2 = bf16[128,256,2]{2,1,0:T(8,128)(2,1)} fusion(bf16[128,256,2,128]{3,2,1,0:T(2,128)(2,1)} %bitcast.123, pred[128,256]{1,0:T(8,128)(4,1)S(1)} %get-tuple-element.18, pred[128,256,128]{2,1,0:T(8,128)(4,1)} %iota_compare_fusion.1), kind=kLoop, calls=%fused_computation.10 | loop fusion | flops 25100288 | bytes 21135360 | tf_op jit(solution)/shard_map/reduce_sum | solution.py:72
  535.3 8.1 fusion.16
  544.2 4.6 fusion.50
  548.9 198.6 %scatter_custom_fusion = f32[16384,128]{1,0:T(8,128)} fusion(s32[32768]{0:T(1024)S(1)} %bitcast.144, f32[]{:T(128)} %constant.93.clone.1, f32[32768]{0:T(1024)S(1)} %bitcast.139, s32[32768]{0:T(1024)S(1)} %bitcast.138), kind=kCustom, calls=%fused_computation.6 | custom fusion | flops 12582912 | bytes 8651776 | tf_op jit(solution)/shard_map/scatter-add | solution.py:81
  747.5 7.7 copy.61
  755.4 25.3 %reduce-scatter.3.cloned.1.call-done = f32[32,2,128,128]{3,2,1,0:T(8,128)} async-done(((f32[64,2,128,128]{3,2,1,0:T(8,128)}), f32[32,2,128,128]{3,2,1,0:T(8,128)}) %reduce-scatter.3.cloned.1.call-update) | async-done | bytes 4194320 | tf_op jit(solution)/shard_map/reduce_scatter | solution.py:28
  781.0 121.2 %reduce-scatter.5.cloned.1.call-done = f32[1,2,128,128]{3,2,1,0:T(8,128)} async-done(((f32[32,2,128,128]{3,2,1,0:T(8,128)}), f32[1,2,128,128]{3,2,1,0:T(8,128)}) %reduce-scatter.5.cloned.1.call-update) | async-done | bytes 131088 | tf_op jit(solution)/shard_map/reduce_scatter | solution.py:28
  902.2 2.2 bitcast_subtract_fusion
  906.3 1.3 dynamic-slice_bitcast_fusion
  908.6 2.1 pad_maximum_fusion
  910.7 41.8 %all-reduce = (f32[5]{0:T(128)S(1)}, f32[3]{0:T(128)S(1)}, f32[5]{0:T(128)S(1)}) all-reduce(f32[5]{0:T(128)S(1)} %neg.22, f32[3]{0:T(128)S(1)} %pad_maximum_fusion, f32[5]{0:T(128)S(1)} %get-tuple-element.8), channel_id=1, replica_groups=mesh['parts'=4,'pts_0'=32,'pts_1'=2] {'pts_0'}, use_global_device_ids=true, to_apply=%region_7.8 | all-reduce | flops 13 | bytes 104 | tf_op jit(solution)/shard_map/psum | solution.py:19
  952.4 36.0 %all-reduce.1 = (f32[5]{0:T(128)S(1)}, f32[3]{0:T(128)S(1)}, f32[5]{0:T(128)S(1)}) all-reduce(f32[5]{0:T(128)S(1)} %get-tuple-element.10, f32[3]{0:T(128)S(1)} %get-tuple-element.11, f32[5]{0:T(128)S(1)} %get-tuple-element.12), channel_id=1, replica_groups=mesh['parts'=4,'pts_0'=32,'pts_1'=2] {'pts_1'}, use_global_device_ids=true, to_apply=%region_8.9 | all-reduce | flops 13 | bytes 104 | tf_op jit(solution)/shard_map/psum | solution.py:19
  989.7 2.4 subtract_multiply_fusion.1
  992.1 65.5 %all-gather.5.cloned.1.call-done = bf16[1,128,128,128]{3,2,0,1:T(8,128)(2,1)} async-done(((bf16[1,2,128,128]{3,2,0,1:T(8,128)(2,1)}), bf16[1,128,128,128]{3,2,0,1:T(8,128)(2,1)}) %all-gather.5.cloned.1.call-update) | async-done | bytes 4194320 | tf_op jit(solution)/shard_map/all_gather | solution.py:89
  1057.5 7.2 convert_bitcast_fusion.1
  1064.8 4.7 copy.65
  1069.4 112.1 %gather_fusion.1 = bf16[32768,128]{1,0:T(8,128)(2,1)} fusion(bf16[16384,128]{1,0:T(8,128)(2,1)} %bitcast.122, s32[32768]{0:T(1024)S(1)} %broadcast_clamp_fusion), kind=kCustom, calls=%fused_computation.1 | custom fusion | bytes 16908288 | tf_op jit(solution)/shard_map/jit(_take)/gather | solution.py:68
  1181.6 15.7 %fusion.4 = bf16[128,256]{1,0:T(8,128)(2,1)S(1)} fusion(bf16[1,128,256,128]{3,2,1,0:T(8,128)(2,1)} %bitcast.124, s32[128,256]{1,0:T(8,128)S(1)} %fusion.32, pred[128,256]{1,0:T(8,128)(4,1)S(1)} %get-tuple-element.18), kind=kLoop, calls=%fused_computation.12 | loop fusion | flops 16744448 | bytes 8617984 | tf_op jit(solution)/shard_map/reduce_sum | solution.py:72
  1197.3 5.6 fusion.35
  1203.0 1.3 fusion.41
  (47 shorter events, 9.4 us)
Async XLA Ops:
  7.2 167.6 %copy-start = (f32[128,128]{1,0:T(8,128)S(1)}, f32[128,128]{1,0:T(8,128)}, u32[]{:S(2)}) copy-start(f32[128,128]{1,0:T(8,128)} %param.13) | copy-start | bytes 196612
  7.2 155.2 %all-gather.3.cloned.1.call-start = ((), (), s32[]{:S(2)}) async-start(), calls=%async_computation.2 | async-start | bytes 8519680 | tf_op jit(solution)/shard_map/all_gather | solution.py:89
  10.6 770.2 %reduce-scatter.3.cloned.1.call-start = ((), (), s32[]{:S(2)}) async-start(), calls=%async_computation.3 | async-start | bytes 12582912 | tf_op jit(solution)/shard_map/reduce_scatter | solution.py:28
  184.6 5.7 copy-start.1
  535.3 8.2 copy-start.7
  755.2 147.0 %copy-start.2 = (f32[2,128,128]{2,1,0:T(8,128)S(1)}, f32[2,128,128]{2,1,0:T(8,128)}, u32[]{:S(2)}) copy-start(f32[2,128,128]{2,1,0:T(8,128)} %param.12) | copy-start | bytes 393220
  755.2 147.0 %copy-start.3 = (f32[2,128,128]{2,1,0:T(8,128)S(1)}, f32[2,128,128]{2,1,0:T(8,128)}, u32[]{:S(2)}) copy-start(f32[2,128,128]{2,1,0:T(8,128)} %param.11) | copy-start | bytes 393220
  755.2 149.2 %copy-start.5 = (f32[128,128]{1,0:T(8,128)S(1)}, f32[128,128]{1,0:T(8,128)}, u32[]{:S(2)}) copy-start(f32[128,128]{1,0:T(8,128)} %param.15) | copy-start | bytes 196612
  755.3 149.5 %copy-start.6 = (f32[128,128]{1,0:T(8,128)S(1)}, f32[128,128]{1,0:T(8,128)}, u32[]{:S(2)}) copy-start(f32[128,128]{1,0:T(8,128)} %param.14) | copy-start | bytes 196612
  755.3 150.6 %copy-start.8 = (f32[5]{0:T(128)S(1)}, f32[5]{0:T(128)}, u32[]{:S(2)}) copy-start(f32[5]{0:T(128)} %param.20) | copy-start | bytes 64
  755.3 146.9 %reduce-scatter.5.cloned.1.call-start = ((), (), s32[]{:S(2)}) async-start(), calls=%async_computation.4 | async-start | bytes 4325376 | tf_op jit(solution)/shard_map/reduce_scatter | solution.py:28
  780.8 276.7 %all-gather.5.cloned.1.call-start = ((), (), s32[]{:S(2)}) async-start(), calls=%async_computation.5 | async-start | bytes 4259840 | tf_op jit(solution)/shard_map/all_gather | solution.py:89
  904.4 165.0 %copy-start.4 = (f32[2,128,128]{2,1,0:T(8,128)}, f32[2,128,128]{2,1,0:T(8,128)S(1)}, u32[]{:S(2)}) copy-start(f32[2,128,128]{2,1,0:T(8,128)S(1)} %get-tuple-element.16) | copy-start | bytes 393220
Sparse Core Ops, SparseCore 0:
  10.7 151.6 all-gather.2
  755.5 25.2 reduce-scatter.2
  783.3 118.8 reduce-scatter.4
  905.9 151.5 all-gather.4
where the time goes:
time: 1220 us; the launch traced here: 1210 us
  local copies, waits for them, and re-layouts  390 us (32%)
  waiting for transfers between devices  351 us (29%)
  other arithmetic  338 us (28%)
  blocking collectives  77.7 us (6%)
  matrix products  39.1 us (3%)
  between operations  15.5 us (1%)
    gather x2, local copies, waits for them, and re-layouts, pick_cells(): taken = jnp.take(grid_rows, row_ids, axis=1)  327 us
    all_gather x2, waiting for transfers between devices, kron_apply(): gathered = lax.all_gather(partial_value, PTS, axis=1, tiled=True)  204 us
    scatter-add x1, other arithmetic, slab_add(): jnp.zeros((row_count * size_y, size_z), jnp.float32).at[target_row]  199 us
    reduce_scatter x2, waiting for transfers between devices, sum_in_order(): tiles = lax.psum_scatter(tiles, axes[k], scatter_dimension=0, tiled=True)  147 us
    reduce_sum x2, other arithmetic, pick_cells(): return jnp.sum(kept.astype(jnp.float32), axis=-1).astype(jnp.bfloat16)  114 us
    psum x2, blocking collectives, by_axis(): array = lax.psum(array, axis)  77.7 us
  transfers between devices with their start and end apart: 4, of which 4 were waited for; matrix products, arithmetic and copies ran while one was open for 2% of the time, Pallas kernels for 0%

commit v1 on v0

v1 whole, which is shorter than its diff:
```python
import jax
import jax.numpy as jnp
from jax import lax
from jax.experimental import pallas as pl
from jax.experimental.pallas import tpu as pltpu
from jax.sharding import Mesh
from jax.sharding import PartitionSpec as P

BOXX = 16
BOXY = 16
BOXZ = 8
NTRIAL = 5
CORES = 2
GROUP = 8
LOADS = 16
FLUSHES = 16
PTS = ("pts_0", "pts_1")
PARTS_PTS = ("parts", "pts_0", "pts_1")

HIGHEST = lax.Precision.HIGHEST
F32 = jnp.float32
BF16 = jnp.bfloat16
I32 = jnp.int32


def plane_mix(fields, kern_y, kern_z):
    inner_mix = jnp.einsum("...bc,zc->...bz", fields, kern_z, precision=HIGHEST)
    return jnp.einsum("...xbz,yb->...xyz", inner_mix, kern_y, precision=HIGHEST).astype(BF16)


def kron_rows(fields, kern_x, kern_y, kern_z, staged):
    count, slab, size_y, size_z = fields.shape
    devices = lax.axis_size(PTS)
    cores = lax.axis_size("pts_1")
    planes = plane_mix(fields, kern_y, kern_z)
    if staged:
        sent = planes.reshape(count, slab, cores, devices // cores, size_y // devices, size_z)
        sent = sent.transpose(3, 2, 0, 1, 4, 5).reshape(devices, count, slab, -1, size_z)
    else:
        sent = planes.reshape(count, slab, devices, size_y // devices, size_z)
        sent = sent.transpose(2, 0, 1, 3, 4)
    got = lax.all_to_all(sent, PTS, 0, 0, tiled=True)
    lines = got.transpose(1, 3, 0, 2, 4).reshape(count, size_y // devices, -1, size_z)
    mixed = jnp.einsum("xa,fyaz->fyxz", kern_x, lines.astype(F32), precision=HIGHEST)
    low = mixed.astype(BF16)
    if staged:
        whole = lax.all_gather(low, "pts_0", axis=0)
        whole = lax.all_gather(whole, "pts_1", axis=0)
        return whole.reshape(devices, *low.shape)
    return lax.all_gather(low, PTS, axis=0)


def depth_lines(corner_z, offsets, size_z):
    line = lax.broadcasted_iota(I32, (size_z, offsets.shape[1]), 0)
    return line == corner_z + (offsets & (BOXZ - 1))


def load_rows(grid_ref, chunk, step):
    devices, count, slab = chunk.shape[:3]
    for d in range(devices):
        for f in range(count):
            for r in range(slab):
                row = (step * devices + d) * slab + r
                grid_ref[f, row] = chunk[d, f, r].astype(F32)


def box_values(grid_ref, corner_ref, block, offsets, depth_mask):
    columns = offsets.shape[1]
    size_z = grid_ref.shape[-1]
    row = ((offsets // BOXZ) & (BOXY - 1)) * BOXX + offsets // (BOXY * BOXZ)
    wanted = lax.broadcasted_iota(I32, (BOXX * BOXY, columns), 0) == row
    pick = jnp.where(depth_mask, 1.0, 0.0).astype(BF16)
    found = []
    for f in range(grid_ref.shape[0]):
        box = grid_ref[f, pl.ds(corner_ref[1, block], BOXY), pl.ds(corner_ref[0, block], BOXX), :]
        box = box.reshape(BOXY * BOXX, size_z).astype(BF16)
        taken = jnp.dot(box, pick, preferred_element_type=F32)
        found.append(jnp.sum(jnp.where(wanted, taken, 0.0), axis=0, keepdims=True))
    return jnp.concatenate(found, axis=0).astype(BF16) if len(found) > 1 else found[0].astype(BF16)


def on_points(values, interp):
    return lax.dot_general(values, interp, (((1,), (1,)), ((), ())), preferred_element_type=F32)


def forward_kernel(
    corner_ref,
    core_ref,
    chosen_ref,
    rows_ref,
    interp_ref,
    offsets_ref,
    labels_ref,
    latent_ref,
    slope_ref,
    own_ref,
    other_ref,
    grid_ref,
    sum_ref,
):
    step = pl.program_id(0)
    steps = pl.num_programs(0)
    size_x = sum_ref.shape[0]
    size_z = sum_ref.shape[-1]

    @pl.when(step < LOADS)
    def _():
        load_rows(grid_ref, rows_ref, step)
        some = size_x // LOADS
        sum_ref[pl.ds(step * some, some)] = jnp.zeros((some, *sum_ref.shape[1:]), F32)

    @pl.when((step >= LOADS) & (step < steps - FLUSHES))
    def _():
        first = (step - LOADS) * GROUP
        masks = []
        points = []
        for k in range(GROUP):
            offsets = offsets_ref[k : k + 1, :]
            mask = depth_lines(corner_ref[2, first + k], offsets, size_z)
            values = box_values(grid_ref, corner_ref, first + k, offsets, mask)
            points.append(on_points(values, interp_ref[k]))
        latent = jnp.concatenate([p[0:1] for p in points], axis=0)
        slope = jnp.concatenate([p[1:2] for p in points], axis=0)
        latent_ref[...] = latent
        slope_ref[...] = slope
        probability = 1.0 / (1.0 + jnp.exp(-(latent + chosen_ref[0] * slope)))
        residual = labels_ref[...].astype(F32) - probability
        for k in range(GROUP):
            offsets = offsets_ref[k : k + 1, :]
            mask = depth_lines(corner_ref[2, first + k], offsets, size_z)
            term = jnp.dot(
                residual[k : k + 1].astype(BF16), interp_ref[k], preferred_element_type=F32
            )
            high = term.astype(BF16).astype(F32)
            low = term - high
            placed = jnp.concatenate(
                [
                    jnp.where(mask, high, 0.0).astype(BF16),
                    jnp.where(mask, low, 0.0).astype(BF16),
                ],
                axis=0,
            )
            row = lax.broadcasted_iota(I32, (BOXX * BOXY, offsets.shape[1]), 0)
            hot = jnp.where(row == offsets // BOXZ, 1.0, 0.0).astype(BF16)
            added = lax.dot_general(
                hot, placed, (((1,), (1,)), ((), ())), preferred_element_type=F32
            )
            added = (added[:, :size_z] + added[:, size_z:]).reshape(BOXX, BOXY, size_z)
            spot = (
                pl.ds(corner_ref[0, first + k], BOXX),
                pl.ds(corner_ref[1, first + k], BOXY),
                slice(None),
            )
            sum_ref[spot] = sum_ref[spot] + added

    half = FLUSHES // CORES
    for part, (spread_ref, core) in enumerate(
        ((other_ref, CORES - 1 - core_ref[0]), (own_ref, core_ref[0]))
    ):
        start = steps - FLUSHES + part * half

        @pl.when((step >= start) & (step < start + half))
        def _():
            chips, slab = spread_ref.shape[:2]
            for c in range(chips):
                for r in range(slab):
                    device = ((step - start) * chips + c) * CORES + core
                    spread_ref[c, r] = sum_ref[device * slab + r]


def bend_kernel(
    corner_ref,
    chosen_ref,
    rows_ref,
    interp_ref,
    offsets_ref,
    latent_ref,
    slope_ref,
    curvature_ref,
    grid_ref,
):
    step = pl.program_id(0)
    size_z = grid_ref.shape[-1]

    @pl.when(step < LOADS)
    def _():
        load_rows(grid_ref, rows_ref, step)

    @pl.when(step >= LOADS)
    def _():
        first = (step - LOADS) * GROUP
        points = []
        for k in range(GROUP):
            offsets = offsets_ref[k : k + 1, :]
            mask = depth_lines(corner_ref[2, first + k], offsets, size_z)
            values = box_values(grid_ref, corner_ref, first + k, offsets, mask)
            points.append(on_points(values, interp_ref[k]))
        bend = jnp.concatenate(points, axis=0)
        probability = 1.0 / (1.0 + jnp.exp(-(latent_ref[...] + chosen_ref[0] * slope_ref[...])))
        curvature_ref[...] = probability * (1.0 - probability) * bend


def run_forward(corner, core, chosen, rows, interp, offsets, labels):
    devices, count, slab, size_x, size_z = rows.shape
    blocks, points, columns = interp.shape
    groups = blocks // GROUP
    load = devices // LOADS
    at = lambda i: jnp.clip(i - LOADS, 0, groups - 1)
    chips = devices // CORES
    half = FLUSHES // CORES
    flush = lambda i, part: (jnp.clip(i - LOADS - groups - part * half, 0, half - 1), 0, 0, 0)
    flush_block = (chips // half, size_x // devices, devices * slab, size_z)
    flushed = jax.ShapeDtypeStruct((chips, *flush_block[1:]), F32)
    point_spec = pl.BlockSpec((GROUP, points), lambda i, *_: (at(i), 0))
    return pl.pallas_call(
        forward_kernel,
        grid_spec=pltpu.PrefetchScalarGridSpec(
            num_scalar_prefetch=3,
            grid=(LOADS + groups + FLUSHES,),
            in_specs=[
                pl.BlockSpec(
                    (load, count, slab, size_x, size_z),
                    lambda i, *_: (jnp.minimum(i, LOADS - 1), 0, 0, 0, 0),
                ),
                pl.BlockSpec((GROUP, points, columns), lambda i, *_: (at(i), 0, 0)),
                pl.BlockSpec((GROUP, columns), lambda i, *_: (at(i), 0)),
                point_spec,
            ],
            out_specs=[
                point_spec,
                point_spec,
                pl.BlockSpec(flush_block, lambda i, *_: flush(i, 1)),
                pl.BlockSpec(flush_block, lambda i, *_: flush(i, 0)),
            ],
            scratch_shapes=[
                pltpu.VMEM((count, devices * slab, size_x, size_z), F32),
                pltpu.VMEM((size_x, devices * slab, size_z), F32),
            ],
        ),
        out_shape=[
            jax.ShapeDtypeStruct((blocks, points), F32),
            jax.ShapeDtypeStruct((blocks, points), F32),
            flushed,
            flushed,
        ],
        name="forward",
    )(corner, core, chosen, rows, interp, offsets, labels)


def run_bend(corner, chosen, rows, interp, offsets, latent, slope):
    devices, count, slab, size_x, size_z = rows.shape
    blocks, points, columns = interp.shape
    groups = blocks // GROUP
    at = lambda i: jnp.maximum(i - LOADS, 0)
    point_spec = pl.BlockSpec((GROUP, points), lambda i, *_: (at(i), 0))
    return pl.pallas_call(
        bend_kernel,
        grid_spec=pltpu.PrefetchScalarGridSpec(
            num_scalar_prefetch=2,
            grid=(LOADS + groups,),
            in_specs=[
                pl.BlockSpec(
                    (devices // LOADS, count, slab, size_x, size_z),
                    lambda i, *_: (jnp.minimum(i, LOADS - 1), 0, 0, 0, 0),
                ),
                pl.BlockSpec((GROUP, points, columns), lambda i, *_: (at(i), 0, 0)),
                pl.BlockSpec((GROUP, columns), lambda i, *_: (at(i), 0)),
                point_spec,
                point_spec,
            ],
            out_specs=point_spec,
            scratch_shapes=[pltpu.VMEM((count, devices * slab, size_x, size_z), F32)],
        ),
        out_shape=jax.ShapeDtypeStruct((blocks, points), F32),
        name="bend",
    )(corner, chosen, rows, interp, offsets, latent, slope)


def body(
    grid_weights,
    direction,
    kern_x,
    kern_y,
    kern_z,
    interp,
    block_corner,
    block_offsets,
    labels,
    trial_steps,
    accept,
):
    slab, size_y, size_z = grid_weights.shape
    devices = lax.axis_size(PTS)
    points = interp.shape[0] * interp.shape[1] * devices
    chosen = jnp.sum(jnp.where(jnp.arange(NTRIAL) == accept[0], trial_steps, 0.0))
    fields = jnp.stack([grid_weights, direction])
    rows = kron_rows(fields, kern_x, kern_y, kern_z, True)
    core = lax.axis_index("pts_1")
    latent, slope_pt, own, other = run_forward(
        block_corner, core[None], chosen[None], rows, interp, block_offsets, labels
    )
    swap = [(c, CORES - 1 - c) for c in range(CORES)]
    part = (own + lax.ppermute(other, "pts_1", swap)).astype(BF16)
    spread = lax.psum_scatter(part, "pts_0", scatter_dimension=0, tiled=True)[0].astype(F32)

    mine = lax.dynamic_slice_in_dim(rows, lax.axis_index(PTS) * slab, slab, 3).astype(F32)
    weights = jnp.stack([grid_weights, direction]).reshape(2, slab, devices, -1, size_z)
    quad = jnp.einsum("gxdyz,dfyxz->gf", weights, mine, precision=HIGHEST)
    target = labels.astype(F32)
    signed = 2.0 * target - 1.0
    trial_latent = latent[None] + trial_steps[:, None, None] * slope_pt[None]
    loglik = jnp.sum(jax.nn.log_sigmoid(signed[None] * trial_latent), axis=(1, 2))
    descent = jnp.sum((target[None] - jax.nn.sigmoid(trial_latent)) * slope_pt[None], axis=(1, 2))
    sums = lax.psum(jnp.concatenate([loglik, descent, quad.reshape(-1)]), PTS)
    loglik = sums[:NTRIAL]
    descent = sums[NTRIAL : 2 * NTRIAL]
    quad_gu, quad_du, quad_dv = sums[2 * NTRIAL], sums[2 * NTRIAL + 2], sums[2 * NTRIAL + 3]
    prior = 0.5 * (quad_gu + 2.0 * trial_steps * quad_du + trial_steps * trial_steps * quad_dv)
    trial_objective = (loglik - prior) / points
    trial_slope = (descent - quad_du - trial_steps * quad_dv) / points

    new_weights = grid_weights + chosen * direction
    grid_gradient = spread - new_weights
    bend_rows = kron_rows(grid_gradient[None], kern_x, kern_y, kern_z, False)
    curvature = run_bend(
        block_corner, chosen[None], bend_rows, interp, block_offsets, latent, slope_pt
    )
    return (new_weights, grid_gradient, curvature, trial_objective, trial_slope)


def solution(mesh):
    parts = mesh.shape["parts"]
    finer = Mesh(mesh.devices.reshape(parts, -1, CORES), ("parts", "pts_0", "pts_1"))
    placed = (
        P(PARTS_PTS, None, None),
        P(PARTS_PTS, None, None),
        P(),
        P(),
        P(),
        P(PARTS_PTS, None, None),
        P(None, PARTS_PTS),
        P(PARTS_PTS, None),
        P(PARTS_PTS, None),
        P(),
        P(),
    )
    return jax.shard_map(
        body,
        mesh=finer,
        in_specs=placed,
        out_specs=(
            P(PARTS_PTS, None, None),
            P(PARTS_PTS, None, None),
            P(PARTS_PTS, None),
            P("parts"),
            P("parts"),
        ),
        check_vma=False,
    )
```

time: 1220 us -> 656 us (0.54)
  local copies, waits for them, and re-layouts: 390 us -> 4.99 us
  other arithmetic: 338 us -> 10.1 us
  blocking collectives: 77.7 us -> 222 us
  Pallas kernels: 0 us -> 108 us
  waiting for transfers between devices: 351 us -> 288 us
  matrix products: 39.1 us -> 5.83 us
    gather x2 -> x0, local copies, waits for them, and re-layouts: 327 us -> none  [pick_cells(): taken = jnp.take(grid_rows, row_ids, axis=1)]
    scatter-add x1 -> x0, other arithmetic: 199 us -> none  [slab_add(): jnp.zeros((row_count * size_y, size_z), jnp.float32).at[target_row]]
    all_to_all x0 -> x2, blocking collectives: none -> 130 us  [kron_rows(): got = lax.all_to_all(sent, PTS, 0, 0, tiled=True)]
    reduce_sum x4 -> x1, other arithmetic: 115 us -> 0.49 us  [body(): jnp.sum(jax.nn.log_sigmoid(signed[None] * trial_latent), axis=(1, 2))]
    pallas_call x0 -> x2, Pallas kernels: none -> 108 us  [the longest x1 69.3 us: run_forward(): pl.pallas_call(forward_kernel, grid_spec=pltpu.PrefetchScalarGridSpec(num...]
    all_gather x2 -> x3, waiting for transfers between devices: 204 us -> 169 us  [the longest x1 101 us: kron_rows(): whole = lax.all_gather(low, 'pts_0', axis=0)]
    reduce_scatter x2 -> x1, waiting for transfers between devices: 147 us -> 112 us  [body(): lax.psum_scatter(part, 'pts_0', scatter_dimension=0, tiled=True)[0]]
    dot_general x5 -> x3, matrix products: 35.3 us -> 2.71 us  [the longest x2 1.43 us: kron_rows(): jnp.einsum('xa,fyaz->fyxz', kern_x, lines.astype(F32), precision=HIGHEST)]
  transfers between devices with their start and end apart: 4 -> 5, of which waited for: 4 -> 5; matrix products, arithmetic and copies ran while one was open for 2% -> 1% of each run, Pallas kernels for 0% -> 0%
where the time goes in v1:
time: 656 us; the launch traced here: 655 us
  waiting for transfers between devices  288 us (44%)
  blocking collectives  222 us (34%)
  Pallas kernels  108 us (16%)
  between operations  15.3 us (2%)
  other arithmetic  10.1 us (2%)
    all_to_all x2, blocking collectives, kron_rows(): got = lax.all_to_all(sent, PTS, 0, 0, tiled=True)  130 us
    reduce_scatter x1, waiting for transfers between devices, body(): lax.psum_scatter(part, 'pts_0', scatter_dimension=0, tiled=True)[0]  112 us
    all_gather x1, waiting for transfers between devices, kron_rows(): whole = lax.all_gather(low, 'pts_0', axis=0)  101 us
    psum x1, blocking collectives, body(): sums = lax.psum(jnp.concatenate([loglik, descent, quad.reshape(-1)]), PTS)  91.8 us
    pallas_call x1, Pallas kernels, run_forward(): pl.pallas_call(forward_kernel, grid_spec=pltpu.PrefetchScalarGridSpec(num...  69.3 us
    all_gather x1, waiting for transfers between devices, kron_rows(): whole = lax.all_gather(whole, 'pts_1', axis=0)  50.2 us
    pallas_call x1, Pallas kernels, run_bend(): pl.pallas_call(bend_kernel, grid_spec=pltpu.PrefetchScalarGridSpec(num_sc...  38.9 us
    all_gather x1, waiting for transfers between devices, kron_rows(): return lax.all_gather(low, PTS, axis=0)  17.5 us
  transfers between devices with their start and end apart: 5, of which 5 were waited for; matrix products, arithmetic and copies ran while one was open for 1% of the time, Pallas kernels for 0%

profile of v1, /device:TPU:37, one launch (start us, length us, event | category | flops | bytes accessed | tf_op | source)
XLA Modules:
  0.0 655.0 jit_solution(17554941388534882340)
XLA Ops:
  7.3 0.8 copy-done
  8.0 1.3 fusion.3
  9.4 1.2 convolution_convert_fusion.1
  10.6 0.1 copy.42
  10.8 0.1 copy.43
  10.9 64.1 %all_to_all.10 = bf16[64,2,2,2,128]{4,3,2,1,0:T(2,128)(2,1)S(1)} all-to-all(bf16[64,2,2,2,128]{4,3,2,1,0:T(2,128)(2,1)S(1)} %copy.43), channel_id=1, replica_groups=mesh['parts'=4,'pts_0'=32,'pts_1'=2] {'pts_0','pts_1'}, dimensions={0} | all-to-all | bytes 262144 | tf_op jit(solution)/shard_map/all_to_all | solution.py:42
  75.1 1.2 fusion
  76.3 0.8 copy.46
  77.2 101.2 %all-gather.7.cloned.1.call-done = bf16[64,2,128,128]{3,2,1,0:T(8,128)(2,1)} async-done(((bf16[2,2,128,128]{3,2,1,0:T(8,128)(2,1)}), bf16[64,2,128,128]{3,2,1,0:T(8,128)(2,1)}) %all-gather.7.cloned.1.call-update) | async-done | bytes 4194320 | tf_op jit(solution)/shard_map/all_gather | solution.py:47
  179.2 0.7 fusion.16
  179.8 50.2 %all-gather.9.cloned.1.call-done.rows_ref = bf16[64,2,2,128,128]{4,3,2,1,0:T(8,128)(2,1)} async-done(((bf16[32,2,2,128,128]{4,3,2,1,0:T(8,128)(2,1)}), bf16[64,2,2,128,128]{4,3,2,1,0:T(8,128)(2,1)}) %all-gather.9.cloned.1.call-update) | async-done | bytes 8388624 | tf_op jit(solution)/shard_map/all_gather | solution.py:48
  230.0 69.3 %forward.1 = (f32[128,128]{1,0:T(8,128)}, f32[128,128]{1,0:T(8,128)}, f32[32,2,128,128]{3,2,1,0:T(8,128)}, f32[32,2,128,128]{3,2,1,0:T(8,128)}) custom-call(s32[3,128]{1,0:T(4,128)} %corner_ref.3, s32[1]{0:T(128)} %bitcast.1.core_ref, f32[1]{0:T(128)} %bitcast.2.chosen_ref, bf16[64,2,2,128,128]{4,3,2,1,0:T(8,128)(2,1)} %all-gather.9.cloned.1.call-done.rows_ref, ...), custom_call_target="tpu_custom_call" | custom-call | tf_op jit(solution)/shard_map/forward/pallas_call | solution.py:215
  299.2 0.2 collective-permute-start
  299.4 7.2 %collective-permute-done = f32[32,2,128,128]{3,2,1,0:T(8,128)S(1)} collective-permute-done((f32[32,2,128,128]{3,2,1,0:T(8,128)}, f32[32,2,128,128]{3,2,1,0:T(8,128)S(1)}, u32[]{:S(2)}, u32[]{:S(2)}) %collective-permute-start) | collective-permute-done | bytes 4194336 | tf_op jit(solution)/shard_map/ppermute | solution.py:303
  306.6 4.2 add_convert_fusion
  311.0 112.1 %reduce-scatter.2.cloned.1.call-done = bf16[1,2,128,128]{3,2,1,0:T(8,128)(2,1)} async-done(((bf16[32,2,128,128]{3,2,1,0:T(8,128)(2,1)}), bf16[1,2,128,128]{3,2,1,0:T(8,128)(2,1)}) %reduce-scatter.2.cloned.1.call-update) | async-done | bytes 65552 | tf_op jit(solution)/shard_map/reduce_scatter | solution.py:304
  423.1 2.1 convert_subtract_fusion
  425.2 0.3 fusion.14
  425.5 0.3 convolution_convert_fusion.3
  425.9 65.9 %all_to_all.11 = bf16[64,1,2,2,128]{4,2,3,1,0:T(2,128)(2,1)S(1)} all-to-all(bf16[64,1,2,2,128]{4,2,3,1,0:T(2,128)(2,1)S(1)} %bitcast.86), channel_id=1, replica_groups=mesh['parts'=4,'pts_0'=32,'pts_1'=2] {'pts_0','pts_1'}, dimensions={0} | all-to-all | bytes 131072 | tf_op jit(solution)/shard_map/all_to_all | solution.py:42
  491.8 0.3 fusion.1
  492.1 0.7 copy.50
  492.9 0.1 copy.52
  493.1 0.1 copy.51
  493.3 1.2 constant_dynamic-slice_fusion
  494.4 1.3 convolution_bitcast_fusion
  495.8 0.5 fusion.2
  496.4 91.8 %psum.7 = f32[14]{0:T(128)S(1)} all-reduce(f32[14]{0:T(128)S(1)} %pad_maximum_fusion.2), channel_id=1, replica_groups=mesh['parts'=4,'pts_0'=32,'pts_1'=2] {'pts_0','pts_1'}, use_global_device_ids=true, to_apply=%region_4.5 | all-reduce | flops 14 | bytes 112 | tf_op jit(solution)/shard_map/psum | solution.py:314
  588.2 0.7 fusion.19
  589.5 2.5 subtract_multiply_fusion
  592.0 17.5 %all-gather.11.cloned.1.call-done = bf16[64,2,128,128]{3,2,1,0:T(8,128)(2,1)} async-done(((bf16[1,2,128,128]{3,2,1,0:T(8,128)(2,1)}), bf16[64,2,128,128]{3,2,1,0:T(8,128)(2,1)}) %all-gather.11.cloned.1.call-update) | async-done | bytes 4194320 | tf_op jit(solution)/shard_map/all_gather | solution.py:50
  609.5 38.9 %bend.1 = f32[128,128]{1,0:T(8,128)} custom-call(s32[3,128]{1,0:T(4,128)} %corner_ref.3, f32[1]{0:T(128)} %bitcast.2.chosen_ref, bf16[64,1,2,128,128]{4,3,2,1,0:T(8,128)(2,1)} %bitcast.76, bf16[128,128,256]{2,1,0:T(8,128)(2,1)} %interp_ref.3, s32[128,256]{1,0:T(8,128)} %offsets_ref.3, f32[128,128]{1,0:T(8,128)} %get-tuple-element.11.latent_ref, ...), custom_call_target="tpu_custom_call" | custom-call | tf_op jit(solution)/shard_map/bend/pallas_call | solution.py:256
  (35 shorter events, 0.9 us)
Async XLA Ops:
  7.2 0.8 copy-start
  7.2 172.0 %copy-start.9 = (f32[5]{0:T(128)S(1)}, f32[5]{0:T(128)}, u32[]{:S(2)}) copy-start(f32[5]{0:T(128)} %param.20) | copy-start | bytes 64
  7.2 171.2 %all-gather.7.cloned.1.call-start = ((), (), s32[]{:S(2)}) async-start(), calls=%async_computation.4 | async-start | bytes 4325376 | tf_op jit(solution)/shard_map/all_gather | solution.py:47
  77.1 152.8 %all-gather.9.cloned.1.call-start = ((), (), s32[]{:S(2)}) async-start(), calls=%async_computation.5 | async-start | bytes 12582912 | tf_op jit(solution)/shard_map/all_gather | solution.py:48
  178.4 244.6 %reduce-scatter.2.cloned.1.call-start = ((), (), s32[]{:S(2)}) async-start(), calls=%async_computation.3 | async-start | bytes 2162688 | tf_op jit(solution)/shard_map/reduce_scatter | solution.py:304
  299.2 7.4 %collective-permute-start = (f32[32,2,128,128]{3,2,1,0:T(8,128)}, f32[32,2,128,128]{3,2,1,0:T(8,128)S(1)}, u32[]{:S(2)}, u32[]{:S(2)}) collective-permute-start(f32[32,2,128,128]{3,2,1,0:T(8,128)} %get-tuple-element.10), channel_id=1, source_target_pairs={{0,1},{1,0},{2,3},{3,2},{4,5},{5,4},{6,7},{7,6},{8,9},{9,8},{10,11... | collective-permute-start | bytes 12582920 | tf_op jit(solution)/shard_map/ppermute | solution.py:303
  306.6 116.5 %copy-start.1 = (f32[2,128,128]{2,1,0:T(8,128)S(1)}, f32[2,128,128]{2,1,0:T(8,128)}, u32[]{:S(2)}) copy-start(f32[2,128,128]{2,1,0:T(8,128)} %param.12) | copy-start | bytes 393220
  306.6 116.5 %copy-start.2 = (f32[2,128,128]{2,1,0:T(8,128)S(1)}, f32[2,128,128]{2,1,0:T(8,128)}, u32[]{:S(2)}) copy-start(f32[2,128,128]{2,1,0:T(8,128)} %param.11) | copy-start | bytes 393220
  306.6 118.9 %copy-start.6 = (f32[128,128]{1,0:T(8,128)S(1)}, f32[128,128]{1,0:T(8,128)}, u32[]{:S(2)}) copy-start(f32[128,128]{1,0:T(8,128)} %param.14) | copy-start | bytes 196612
  306.6 185.2 %copy-start.5 = (f32[128,128]{1,0:T(8,128)S(1)}, f32[128,128]{1,0:T(8,128)}, u32[]{:S(2)}) copy-start(f32[128,128]{1,0:T(8,128)} %param.13) | copy-start | bytes 196612
  306.6 186.3 %copy-start.3 = (s32[128,128]{1,0:T(8,128)S(1)}, s32[128,128]{1,0:T(8,128)}, u32[]{:S(2)}) copy-start(s32[128,128]{1,0:T(8,128)} %labels_ref.1) | copy-start | bytes 196612
  310.8 185.0 %copy-start.7 = (f32[128,128]{1,0:T(8,128)S(1)}, f32[128,128]{1,0:T(8,128)}, u32[]{:S(2)}) copy-start(f32[128,128]{1,0:T(8,128)} %get-tuple-element.11.latent_ref) | copy-start | bytes 196612
  310.8 185.0 %copy-start.8 = (f32[128,128]{1,0:T(8,128)S(1)}, f32[128,128]{1,0:T(8,128)}, u32[]{:S(2)}) copy-start(f32[128,128]{1,0:T(8,128)} %get-tuple-element.12.slope_ref) | copy-start | bytes 196612
  310.9 298.7 %all-gather.11.cloned.1.call-start = ((), (), s32[]{:S(2)}) async-start(), calls=%async_computation.6 | async-start | bytes 4259840 | tf_op jit(solution)/shard_map/all_gather | solution.py:50
  425.2 223.2 %copy-start.4 = (f32[2,128,128]{2,1,0:T(8,128)}, f32[2,128,128]{2,1,0:T(8,128)S(1)}, u32[]{:S(2)}) copy-start(f32[2,128,128]{2,1,0:T(8,128)S(1)} %get-tuple-element.15) | copy-start | bytes 393220
Sparse Core Ops, SparseCore 0:
  77.3 101.0 all-gather.6
  180.2 49.7 all-gather.8
  311.0 112.0 reduce-scatter.1
  493.0 116.4 all-gather.10

commit v2 on v1

v2 whole, which is shorter than its diff:
```python
import jax
import jax.numpy as jnp
from jax import lax
from jax.experimental import pallas as pl
from jax.experimental.pallas import tpu as pltpu
from jax.sharding import Mesh
from jax.sharding import PartitionSpec as P

BOXX = 16
BOXY = 16
BOXZ = 8
NTRIAL = 5
CORES = 2
GROUP = 8
LOADS = 16
FLUSHES = 16
MIXES = 16
PTS = ("pts_0", "pts_1")
PARTS_PTS = ("parts", "pts_0", "pts_1")

HIGHEST = lax.Precision.HIGHEST
F32 = jnp.float32
BF16 = jnp.bfloat16
I32 = jnp.int32


def plane_mix(fields, kern_y, kern_z):
    inner_mix = jnp.einsum("...bc,zc->...bz", fields, kern_z, precision=HIGHEST)
    return jnp.einsum("...xbz,yb->...xyz", inner_mix, kern_y, precision=HIGHEST).astype(BF16)


def pieces_of(array):
    high = lax.reduce_precision(array, 8, 7)
    rest = array - high
    middle = lax.reduce_precision(rest, 8, 7)
    return high.astype(BF16), middle.astype(BF16), (rest - middle).astype(BF16)


def depth_lines(corner_z, offsets, size_z):
    line = lax.broadcasted_iota(I32, (size_z, offsets.shape[1]), 0)
    return line == corner_z + (offsets & (BOXZ - 1))


def load_planes(plane_ref, chunk, step, slab_rows):
    devices = chunk.shape[0]
    for d in range(devices):
        first = pl.multiple_of((step * devices + d) * slab_rows, slab_rows)
        plane_ref[pl.ds(first, slab_rows), :] = chunk[d, :slab_rows].astype(F32)


def mix_planes(grid_ref, plane_ref, kern, step, size_x, size_y):
    some = size_y // MIXES
    size_z = grid_ref.shape[-1]
    for k in range(0, some, 2):
        row = step * some + k
        pair = [plane_ref[pl.ds(row + r, size_x, stride=size_y), :].astype(BF16) for r in range(2)]
        mixed = jnp.dot(kern, jnp.concatenate(pair, axis=1), preferred_element_type=F32)
        mixed = mixed[:size_x] + mixed[size_x : 2 * size_x] + mixed[2 * size_x :]
        for r in range(2):
            first = pl.multiple_of((row + r) * size_x, size_x)
            grid_ref[pl.ds(first, size_x), :] = mixed[:, r * size_z : (r + 1) * size_z]


def prepare(step, kern_ref, rows_ref, plane_ref, grid_ref):
    size_x = kern_ref.shape[1]
    size_y = plane_ref.shape[0] // size_x
    slab_rows = plane_ref.shape[0] // (LOADS * rows_ref.shape[0])

    @pl.when(step < LOADS)
    def _():
        load_planes(plane_ref, rows_ref, step, slab_rows)

    @pl.when((step >= LOADS) & (step < LOADS + MIXES))
    def _():
        mix_planes(grid_ref, plane_ref, kern_ref[...], step - LOADS, size_x, size_y)


def own_planes(image_ref, grid_ref, device, size_x):
    slab, size_y = image_ref.shape[:2]
    for r in range(slab):
        image_ref[r] = grid_ref[pl.ds(device * slab + r, size_y, stride=size_x), :]


def box_values(grid_ref, corner_ref, block, offsets, depth_mask, size_x):
    row = ((offsets // BOXZ) & (BOXY - 1)) * BOXX + offsets // (BOXY * BOXZ)
    wanted = lax.broadcasted_iota(I32, (BOXX * BOXY, offsets.shape[1]), 0) == row
    pick = jnp.where(depth_mask, 1.0, 0.0).astype(BF16)
    first = corner_ref[1, block] * size_x + corner_ref[0, block]
    box = [grid_ref[pl.ds(first + k * size_x, BOXX), :].astype(BF16) for k in range(BOXY)]
    taken = jnp.dot(jnp.concatenate(box, axis=0), pick, preferred_element_type=F32)
    return jnp.sum(jnp.where(wanted, taken, 0.0), axis=0, keepdims=True).astype(BF16)


def on_points(values, interp):
    return lax.dot_general(values, interp, (((1,), (1,)), ((), ())), preferred_element_type=F32)


def field_points(first, corner_ref, offsets_ref, interp_ref, grid_ref, size_x):
    points = []
    for k in range(GROUP):
        offsets = offsets_ref[k : k + 1, :]
        mask = depth_lines(corner_ref[2, first + k], offsets, grid_ref.shape[-1])
        values = box_values(grid_ref, corner_ref, first + k, offsets, mask, size_x)
        points.append(on_points(values, interp_ref[k]))
    return jnp.concatenate(points, axis=0)


def latent_kernel(
    corner_ref,
    place_ref,
    chosen_ref,
    kern_ref,
    rows_ref,
    interp_ref,
    offsets_ref,
    latent_ref,
    image_ref,
    plane_ref,
    grid_ref,
):
    step = pl.program_id(0)
    size_x = kern_ref.shape[1]
    prepare(step, kern_ref, rows_ref, plane_ref, grid_ref)

    @pl.when(step == LOADS + MIXES)
    def _():
        own_planes(image_ref, grid_ref, place_ref[1], size_x)

    @pl.when(step >= LOADS + MIXES)
    def _():
        first = (step - LOADS - MIXES) * GROUP
        latent_ref[...] = field_points(
            first, corner_ref, offsets_ref, interp_ref, grid_ref, size_x
        )


def bend_kernel(
    corner_ref,
    place_ref,
    chosen_ref,
    kern_ref,
    rows_ref,
    interp_ref,
    offsets_ref,
    latent_ref,
    slope_ref,
    curvature_ref,
    plane_ref,
    grid_ref,
):
    step = pl.program_id(0)
    prepare(step, kern_ref, rows_ref, plane_ref, grid_ref)

    @pl.when(step >= LOADS + MIXES)
    def _():
        first = (step - LOADS - MIXES) * GROUP
        bend = field_points(
            first, corner_ref, offsets_ref, interp_ref, grid_ref, kern_ref.shape[1]
        )
        probability = 1.0 / (1.0 + jnp.exp(-(latent_ref[...] + chosen_ref[0] * slope_ref[...])))
        curvature_ref[...] = probability * (1.0 - probability) * bend


def spread_kernel(
    corner_ref,
    place_ref,
    chosen_ref,
    kern_ref,
    rows_ref,
    interp_ref,
    offsets_ref,
    labels_ref,
    latent_ref,
    slope_ref,
    turn_ref,
    own_ref,
    other_ref,
    plane_ref,
    grid_ref,
    sum_ref,
):
    step = pl.program_id(0)
    steps = pl.num_programs(0)
    size_x = sum_ref.shape[0]
    size_z = sum_ref.shape[-1]
    prepare(step, kern_ref, rows_ref, plane_ref, grid_ref)

    @pl.when(step < LOADS)
    def _():
        some = size_x // LOADS
        sum_ref[pl.ds(step * some, some)] = jnp.zeros((some, *sum_ref.shape[1:]), F32)

    @pl.when(step == LOADS + MIXES)
    def _():
        own_planes(turn_ref, grid_ref, place_ref[1], size_x)

    @pl.when((step >= LOADS + MIXES) & (step < steps - FLUSHES))
    def _():
        first = (step - LOADS - MIXES) * GROUP
        slope = field_points(first, corner_ref, offsets_ref, interp_ref, grid_ref, size_x)
        slope_ref[...] = slope
        probability = 1.0 / (1.0 + jnp.exp(-(latent_ref[...] + chosen_ref[0] * slope)))
        residual = labels_ref[...].astype(F32) - probability
        for k in range(GROUP):
            offsets = offsets_ref[k : k + 1, :]
            mask = depth_lines(corner_ref[2, first + k], offsets, size_z)
            term = jnp.dot(
                residual[k : k + 1].astype(BF16), interp_ref[k], preferred_element_type=F32
            )
            high = term.astype(BF16).astype(F32)
            low = term - high
            placed = jnp.concatenate(
                [
                    jnp.where(mask, high, 0.0).astype(BF16),
                    jnp.where(mask, low, 0.0).astype(BF16),
                ],
                axis=0,
            )
            row = lax.broadcasted_iota(I32, (BOXX * BOXY, offsets.shape[1]), 0)
            hot = jnp.where(row == offsets // BOXZ, 1.0, 0.0).astype(BF16)
            added = lax.dot_general(
                hot, placed, (((1,), (1,)), ((), ())), preferred_element_type=F32
            )
            added = (added[:, :size_z] + added[:, size_z:]).reshape(BOXX, BOXY, size_z)
            spot = (
                pl.ds(corner_ref[0, first + k], BOXX),
                pl.ds(corner_ref[1, first + k], BOXY),
                slice(None),
            )
            sum_ref[spot] = sum_ref[spot] + added

    half = FLUSHES // CORES
    for part, (out_ref, core) in enumerate(
        ((other_ref, CORES - 1 - place_ref[0]), (own_ref, place_ref[0]))
    ):
        start = steps - FLUSHES + part * half

        @pl.when((step >= start) & (step < start + half))
        def _():
            chips, slab = out_ref.shape[:2]
            for c in range(chips):
                for r in range(slab):
                    device = ((step - start) * chips + c) * CORES + core
                    out_ref[c, r] = sum_ref[device * slab + r]


def run(kernel, name, scalars, kern, rows, interp, offsets, extra, slab, size_y):
    devices = rows.shape[0]
    size_z = rows.shape[2]
    size_x = slab * devices
    blocks, points, columns = interp.shape
    groups = blocks // GROUP
    before = LOADS + MIXES
    at = lambda i: jnp.clip(i - before, 0, groups - 1)
    whole = lambda *shape: pl.BlockSpec(shape, lambda i, *_: (0,) * len(shape))
    point_spec = pl.BlockSpec((GROUP, points), lambda i, *_: (at(i), 0))
    point_shape = jax.ShapeDtypeStruct((blocks, points), F32)
    image_spec = whole(slab, size_y, size_z)
    image_shape = jax.ShapeDtypeStruct((slab, size_y, size_z), F32)
    scratch = [pltpu.VMEM((size_x * size_y, size_z), F32) for _ in range(2)]
    steps = before + groups
    if kernel is bend_kernel:
        out_specs, out_shape = point_spec, point_shape
    elif kernel is latent_kernel:
        out_specs, out_shape = [point_spec, image_spec], [point_shape, image_shape]
    else:
        half = FLUSHES // CORES
        chips = devices // CORES
        block = (chips // half, slab, size_y, size_z)
        flush = lambda part: pl.BlockSpec(
            block, lambda i, *_: (jnp.clip(i - steps - part * half, 0, half - 1), 0, 0, 0)
        )
        flushed = jax.ShapeDtypeStruct((chips, slab, size_y, size_z), F32)
        out_specs = [point_spec, image_spec, flush(1), flush(0)]
        out_shape = [point_shape, image_shape, flushed, flushed]
        scratch.append(pltpu.VMEM((size_x, size_y, size_z), F32))
    return pl.pallas_call(
        kernel,
        grid_spec=pltpu.PrefetchScalarGridSpec(
            num_scalar_prefetch=3,
            grid=(steps + (FLUSHES if kernel is spread_kernel else 0),),
            in_specs=[
                whole(*kern.shape),
                pl.BlockSpec(
                    (devices // LOADS, *rows.shape[1:]),
                    lambda i, *_: (jnp.minimum(i, LOADS - 1), 0, 0),
                ),
                pl.BlockSpec((GROUP, points, columns), lambda i, *_: (at(i), 0, 0)),
                pl.BlockSpec((GROUP, columns), lambda i, *_: (at(i), 0)),
                *[point_spec for _ in extra],
            ],
            out_specs=out_specs,
            scratch_shapes=scratch,
        ),
        out_shape=out_shape,
        name=name,
    )(*scalars, kern, rows, interp, offsets, *extra)


def body(
    grid_weights,
    direction,
    kern_x,
    kern_y,
    kern_z,
    interp,
    block_corner,
    block_offsets,
    labels,
    trial_steps,
    accept,
):
    slab, size_y, size_z = grid_weights.shape
    devices = lax.axis_size(PTS)
    points = interp.shape[0] * interp.shape[1] * devices
    chosen = jnp.sum(jnp.where(jnp.arange(NTRIAL) == accept[0], trial_steps, 0.0))
    core = lax.axis_index("pts_1")
    kern = jnp.concatenate(pieces_of(kern_x), axis=0)
    scalars = (block_corner, jnp.stack([core, lax.axis_index(PTS)]), chosen[None])
    common = (interp, block_offsets)

    def gathered(field, more=()):
        planes = plane_mix(field, kern_y, kern_z).reshape(slab * size_y, size_z)
        return lax.all_gather(jnp.concatenate([planes, *more], axis=0), PTS, axis=0)

    weight_rows = gathered(grid_weights)
    turn_rows = gathered(direction)
    latent, image = run(
        latent_kernel, "latent", scalars, kern, weight_rows, *common, (), slab, size_y
    )
    slope_pt, turn, own, other = run(
        spread_kernel, "spread", scalars, kern, turn_rows, *common, (labels, latent), slab, size_y
    )
    swap = [(c, CORES - 1 - c) for c in range(CORES)]
    part = (own + lax.ppermute(other, "pts_1", swap)).astype(BF16)
    spread = lax.psum_scatter(part, "pts_0", scatter_dimension=0, tiled=True)[0].astype(F32)

    target = labels.astype(F32)
    signed = 2.0 * target - 1.0
    trial_latent = latent[None] + trial_steps[:, None, None] * slope_pt[None]
    loglik = jnp.sum(jax.nn.log_sigmoid(signed[None] * trial_latent), axis=(1, 2))
    descent = jnp.sum((target[None] - jax.nn.sigmoid(trial_latent)) * slope_pt[None], axis=(1, 2))
    quad = [
        jnp.sum(grid_weights * image),
        jnp.sum(direction * image),
        jnp.sum(direction * turn),
    ]
    local = jnp.concatenate([loglik, descent, jnp.stack(quad)])
    riding = jnp.stack(pieces_of(local))
    riding = jnp.pad(riding, ((0, 16 - riding.shape[0]), (0, size_z - riding.shape[1])))

    new_weights = grid_weights + chosen * direction
    grid_gradient = spread - new_weights
    bend_rows = gathered(grid_gradient, (riding,))
    curvature = run(
        bend_kernel, "bend", scalars, kern, bend_rows, *common, (latent, slope_pt), slab, size_y
    )

    told = bend_rows[:, slab * size_y : slab * size_y + 3, : local.shape[0]]
    sums = jnp.sum(told.astype(F32), axis=(0, 1))
    loglik = sums[:NTRIAL]
    descent = sums[NTRIAL : 2 * NTRIAL]
    quad_gu, quad_du, quad_dv = sums[2 * NTRIAL], sums[2 * NTRIAL + 1], sums[2 * NTRIAL + 2]
    prior = 0.5 * (quad_gu + 2.0 * trial_steps * quad_du + trial_steps * trial_steps * quad_dv)
    trial_objective = (loglik - prior) / points
    trial_slope = (descent - quad_du - trial_steps * quad_dv) / points
    return (new_weights, grid_gradient, curvature, trial_objective, trial_slope)


def solution(mesh):
    parts = mesh.shape["parts"]
    finer = Mesh(mesh.devices.reshape(parts, -1, CORES), ("parts", "pts_0", "pts_1"))
    placed = (
        P(PARTS_PTS, None, None),
        P(PARTS_PTS, None, None),
        P(),
        P(),
        P(),
        P(PARTS_PTS, None, None),
        P(None, PARTS_PTS),
        P(PARTS_PTS, None),
        P(PARTS_PTS, None),
        P(),
        P(),
    )
    return jax.shard_map(
        body,
        mesh=finer,
        in_specs=placed,
        out_specs=(
            P(PARTS_PTS, None, None),
            P(PARTS_PTS, None, None),
            P(PARTS_PTS, None),
            P("parts"),
            P("parts"),
        ),
        check_vma=False,
    )
```

time: 656 us -> 704 us (1.073)
  blocking collectives: 222 us -> 0 us
  waiting for transfers between devices: 288 us -> 483 us
  Pallas kernels: 108 us -> 179 us
    all_gather x3, waiting for transfers between devices: 169 us -> 373 us  [gathered(): return lax.all_gather(jnp.concatenate([planes, *more], axis=0), PTS, axis=0)]
    all_to_all x2 -> x0, blocking collectives: 130 us -> none  [kron_rows(): got = lax.all_to_all(sent, PTS, 0, 0, tiled=True)]
    psum x1 -> x0, blocking collectives: 91.8 us -> none  [body(): sums = lax.psum(jnp.concatenate([loglik, descent, quad.reshape(-1)]), PTS)]
    pallas_call x2 -> x3, Pallas kernels: 108 us -> 179 us  [run(): pl.pallas_call(kernel, grid_spec=pltpu.PrefetchScalarGridSpec(num_scalar_...]
    reduce_scatter x1, waiting for transfers between devices: 112 us -> 103 us  [body(): lax.psum_scatter(part, 'pts_0', scatter_dimension=0, tiled=True)[0]]
  transfers between devices with their start and end apart: 5 -> 5, of which waited for: 5 -> 5; matrix products, arithmetic and copies ran while one was open for 1% -> 1% of each run, Pallas kernels for 0% -> 7%
where the time goes in v2:
time: 704 us; the launch traced here: 703 us
  waiting for transfers between devices  483 us (69%)
  Pallas kernels  179 us (25%)
  other arithmetic  15.4 us (2%)
  between operations  15.2 us (2%)
    all_gather x3, waiting for transfers between devices, gathered(): return lax.all_gather(jnp.concatenate([planes, *more], axis=0), PTS, axis=0)  373 us
    pallas_call x3, Pallas kernels, run(): pl.pallas_call(kernel, grid_spec=pltpu.PrefetchScalarGridSpec(num_scalar_...  179 us
    reduce_scatter x1, waiting for transfers between devices, body(): lax.psum_scatter(part, 'pts_0', scatter_dimension=0, tiled=True)[0]  103 us
  transfers between devices with their start and end apart: 5, of which 5 were waited for; matrix products, arithmetic and copies ran while one was open for 1% of the time, Pallas kernels for 7%

profile of v2, /device:TPU:37, one launch (start us, length us, event | category | flops | bytes accessed | tf_op | source)
XLA Modules:
  0.0 703.2 jit_solution(7460153223568983052)
XLA Ops:
  7.2 0.1 all-gather.7.cloned.1.call-start
  7.3 0.8 copy-done
  8.0 1.2 fusion.7
  9.2 1.7 convolution_convert_fusion.1
  11.0 0.1 all-gather.5.cloned.1.call-start
  11.1 1.2 fusion.9
  12.3 1.7 convolution_convert_fusion.2
  14.1 0.1 reduce-scatter.2.cloned.1.call-start
  14.8 0.6 pad_add_fusion.place_ref
  15.4 1.3 fusion.21
  16.7 0.9 reduce-precision_convert_fusion.1
  17.5 0.6 pad_maximum_fusion.kern_ref
  18.2 140.2 %all-gather.7.cloned.1.call-done.rows_ref = bf16[64,256,128]{2,1,0:T(8,128)(2,1)} async-done(((bf16[1,256,128]{2,1,0:T(8,128)(2,1)}), bf16[64,256,128]{2,1,0:T(8,128)(2,1)}) %all-gather.7.cloned.1.call-update) | async-done | bytes 4194320 | tf_op jit(solution)/shard_map/all_gather | solution.py:324
  158.4 48.6 %latent.1 = (f32[128,128]{1,0:T(8,128)}, f32[2,128,128]{2,1,0:T(8,128)}) custom-call(s32[3,128]{1,0:T(4,128)} %corner_ref.5, s32[2]{0:T(128)} %pad_add_fusion.place_ref, f32[1]{0:T(128)} %bitcast.3.chosen_ref, bf16[384,128]{1,0:T(8,128)(2,1)} %pad_maximum_fusion.kern_ref, bf16[64,256,128]{2,1,0:T(8,128)(2,1)} %all-gather.7.cloned.1.call-done.rows_ref, ...), custom_call_target="tpu_custom_call" | custom-call | tf_op jit(solution)/shard_map/latent/pallas_call | solution.py:277
  207.0 79.6 %all-gather.5.cloned.1.call-done.rows_ref = bf16[64,256,128]{2,1,0:T(8,128)(2,1)} async-done(((bf16[1,256,128]{2,1,0:T(8,128)(2,1)}), bf16[64,256,128]{2,1,0:T(8,128)(2,1)}) %all-gather.5.cloned.1.call-update) | async-done | bytes 4194320 | tf_op jit(solution)/shard_map/all_gather | solution.py:324
  286.6 81.8 %spread.1 = (f32[128,128]{1,0:T(8,128)}, f32[2,128,128]{2,1,0:T(8,128)}, f32[32,2,128,128]{3,2,1,0:T(8,128)}, f32[32,2,128,128]{3,2,1,0:T(8,128)}) custom-call(s32[3,128]{1,0:T(4,128)} %corner_ref.5, s32[2]{0:T(128)} %pad_add_fusion.place_ref, f32[1]{0:T(128)} %bitcast.3.chosen_ref, bf16[384,128]{1,0:T(8,128)(2,1)} %pad_maximum_fusion.kern_ref, ...), custom_call_target="tpu_custom_call" | custom-call | tf_op jit(solution)/shard_map/spread/pallas_call | solution.py:277
  368.4 0.3 collective-permute-start
  368.7 7.1 %collective-permute-done = f32[32,2,128,128]{3,2,1,0:T(8,128)S(1)} collective-permute-done((f32[32,2,128,128]{3,2,1,0:T(8,128)}, f32[32,2,128,128]{3,2,1,0:T(8,128)S(1)}, u32[]{:S(2)}, u32[]{:S(2)}) %collective-permute-start) | collective-permute-done | bytes 4194336 | tf_op jit(solution)/shard_map/ppermute | solution.py:335
  375.8 4.5 add_convert_fusion
  380.4 0.1 all-gather.9.cloned.1.call-start
  380.5 0.5 multiply_reduce_fusion
  381.0 102.9 %reduce-scatter.2.cloned.1.call-done = bf16[1,2,128,128]{3,2,1,0:T(8,128)(2,1)} async-done(((bf16[32,2,128,128]{3,2,1,0:T(8,128)(2,1)}), bf16[1,2,128,128]{3,2,1,0:T(8,128)(2,1)}) %reduce-scatter.2.cloned.1.call-update) | async-done | bytes 65552 | tf_op jit(solution)/shard_map/reduce_scatter | solution.py:336
  483.9 2.9 multiply_reduce_fusion.1
  486.8 2.1 concatenate.49
  488.8 0.3 fusion.5
  489.1 0.3 convolution_convert_fusion
  489.4 0.6 pad_maximum_fusion.1
  490.1 153.3 %all-gather.9.cloned.1.call-done = bf16[17408,128]{1,0:T(8,128)(2,1)} async-done(((bf16[272,128]{1,0:T(8,128)(2,1)}), bf16[17408,128]{1,0:T(8,128)(2,1)}) %all-gather.9.cloned.1.call-update) | async-done | bytes 4456464 | tf_op jit(solution)/shard_map/all_gather | solution.py:324
  643.4 48.5 %bend.1 = f32[128,128]{1,0:T(8,128)} custom-call(s32[3,128]{1,0:T(4,128)} %corner_ref.5, s32[2]{0:T(128)} %pad_add_fusion.place_ref, f32[1]{0:T(128)} %bitcast.3.chosen_ref, bf16[384,128]{1,0:T(8,128)(2,1)} %pad_maximum_fusion.kern_ref, bf16[64,272,128]{2,1,0:T(8,128)(2,1)} %bitcast.47, bf16[128,128,256]{2,1,0:T(8,128)(2,1)} %interp_ref.5, ...), custom_call_target="tpu_custom_call" | custom-call | tf_op jit(solution)/shard_map/bend/pallas_call | solution.py:277
  691.9 1.0 convert_reduce_fusion
  692.9 0.7 fusion.22
  694.2 2.5 subtract_multiply_fusion
  (30 shorter events, 0.3 us)
Async XLA Ops:
  7.2 0.8 copy-start
  7.2 151.2 %all-gather.7.cloned.1.call-start = ((), (), s32[]{:S(2)}) async-start(), calls=%async_computation.2 | async-start | bytes 4259840 | tf_op jit(solution)/shard_map/all_gather | solution.py:324
  11.0 275.6 %all-gather.5.cloned.1.call-start = ((), (), s32[]{:S(2)}) async-start(), calls=%async_computation.1 | async-start | bytes 4259840 | tf_op jit(solution)/shard_map/all_gather | solution.py:324
  14.1 469.8 %reduce-scatter.2.cloned.1.call-start = ((), (), s32[]{:S(2)}) async-start(), calls=%async_computation.3 | async-start | bytes 2162688 | tf_op jit(solution)/shard_map/reduce_scatter | solution.py:336
  368.4 7.4 %collective-permute-start = (f32[32,2,128,128]{3,2,1,0:T(8,128)}, f32[32,2,128,128]{3,2,1,0:T(8,128)S(1)}, u32[]{:S(2)}, u32[]{:S(2)}) collective-permute-start(f32[32,2,128,128]{3,2,1,0:T(8,128)} %get-tuple-element.13), channel_id=1, source_target_pairs={{0,1},{1,0},{2,3},{3,2},{4,5},{5,4},{6,7},{7,6},{8,9},{9,8},{10,11... | collective-permute-start | bytes 12582920 | tf_op jit(solution)/shard_map/ppermute | solution.py:335
  375.8 4.7 copy-start.1
  375.8 4.7 copy-start.6
  375.8 4.8 copy-start.9
  375.8 4.8 copy-start.10
  375.8 108.1 %copy-start.3 = (f32[2,128,128]{2,1,0:T(8,128)S(1)}, f32[2,128,128]{2,1,0:T(8,128)}, u32[]{:S(2)}) copy-start(f32[2,128,128]{2,1,0:T(8,128)} %param.12) | copy-start | bytes 393220
  375.8 108.1 %copy-start.4 = (f32[2,128,128]{2,1,0:T(8,128)S(1)}, f32[2,128,128]{2,1,0:T(8,128)}, u32[]{:S(2)}) copy-start(f32[2,128,128]{2,1,0:T(8,128)} %param.11) | copy-start | bytes 393220
  375.8 108.1 %copy-start.7 = (f32[2,128,128]{2,1,0:T(8,128)S(1)}, f32[2,128,128]{2,1,0:T(8,128)}, u32[]{:S(2)}) copy-start(f32[2,128,128]{2,1,0:T(8,128)} %get-tuple-element.15) | copy-start | bytes 393220
  375.8 108.1 %copy-start.8 = (f32[2,128,128]{2,1,0:T(8,128)S(1)}, f32[2,128,128]{2,1,0:T(8,128)}, u32[]{:S(2)}) copy-start(f32[2,128,128]{2,1,0:T(8,128)} %get-tuple-element.16) | copy-start | bytes 393220
  375.8 113.3 %copy-start.2 = (f32[128,128]{1,0:T(8,128)S(1)}, f32[128,128]{1,0:T(8,128)}, u32[]{:S(2)}) copy-start(f32[128,128]{1,0:T(8,128)} %param.14) | copy-start | bytes 196612
  380.4 263.0 %all-gather.9.cloned.1.call-start = ((), (), s32[]{:S(2)}) async-start(), calls=%async_computation.4 | async-start | bytes 4526080 | tf_op jit(solution)/shard_map/all_gather | solution.py:324
  486.8 205.1 %copy-start.5 = (f32[2,128,128]{2,1,0:T(8,128)}, f32[2,128,128]{2,1,0:T(8,128)S(1)}, u32[]{:S(2)}) copy-start(f32[2,128,128]{2,1,0:T(8,128)S(1)} %get-tuple-element.24) | copy-start | bytes 393220
Sparse Core Ops, SparseCore 0:
  11.1 147.2 all-gather.6
  160.8 125.7 all-gather.4
  380.5 103.3 reduce-scatter.1
  490.3 153.0 all-gather.8
